TPU v7x, 8 devices: a whole 2x2x1 slice. The times are simulated.
8 devices in a mesh: dp: 2 (over z, y), gp: 4 (over x, core).
Axes of the slice: x: 2, y: 2, z: 1, core: 2. Of those that a mesh axis runs over, the one named last changes fastest.
Arguments:
- x_prev: float32 [32768, 83], P(('dp', 'gp')), parts along dimension 0
- x_cur: float32 [32768, 83], P(('dp', 'gp')), parts along dimension 0
- forcing: float32 [32768, 2, 5], P(('dp', 'gp')), parts along dimension 0
- grid_static: float32 [32768, 5], P(('dp', 'gp')), parts along dimension 0
- g2m_feat: float32 [32768, 4], P(('dp', 'gp')), parts along dimension 0
- m2g_feat: float32 [32768, 4], P(('dp', 'gp')), parts along dimension 0
- mesh_feat: float32 [8192, 3], P(('dp', 'gp')), parts along dimension 0
- mesh_edge_feat: float32 [8192, 6, 4], P(('dp', 'gp')), parts along dimension 0
- norm_stats: float32 [4, 83], replicated
- w_grid_in: bfloat16 [176, 512], replicated
- w_mesh_in: bfloat16 [3, 512], replicated
- w_eemb_in: bfloat16 [3, 4, 512], replicated
- w_embed_out: bfloat16 [5, 512, 512], replicated
- w_edge_in: bfloat16 [14, 1536, 512], replicated
- w_edge_out: bfloat16 [14, 512, 512], replicated
- w_node_in: bfloat16 [14, 1024, 512], replicated
- w_node_out: bfloat16 [14, 512, 512], replicated
- w_grid_self: bfloat16 [2, 512, 512], replicated
- w_out_hidden: bfloat16 [512, 512], replicated
- w_out_final: bfloat16 [512, 83], replicated
Outputs:
- output 1: float32 [32768, 83], P(('dp', 'gp')), parts along dimension 0
- output 2: float32 [32768, 83], P(('dp', 'gp')), parts along dimension 0
There are 2 independent parts. A program takes and returns all parts, laid end to end along the dimension named above; an argument that names none is the same for every part.
All inputs are finite; a program needn't handle non-finite values.
Results may differ from a plain program's by a relative error of at most 0.00789786.
Values are sent between devices in bfloat16 or wider.
A program may use at most 1 GiB of HBM per device.

v0:
```python
import functools

import jax
import jax.numpy as jnp
from jax import lax
from jax.experimental import pallas as pl
from jax.experimental.pallas import tpu as pltpu
from jax.sharding import PartitionSpec as P

F32 = jnp.float32
BF16 = jnp.bfloat16
LAT = 512
VARS = 83
LANES = 128
CELLS = 128
RATIO = 4
ROWS = CELLS * RATIO
SUB = 2
Q = 8
RLOC = 128
NODES = Q * RLOC
OFFS = 6
LAYERS = 12
TILE = 256
CHUNK = 512
LAG_B = 1
LAG_C = 2
VMEM_LIMIT = 60 * 1024 * 1024


def mm(lhs, rhs):
    return jnp.dot(lhs, rhs, preferred_element_type=F32)


def silu_twice(x):
    return (x + x * jnp.tanh(x)).astype(BF16)


def half_norm(y):
    centred = y - jnp.sum(y, axis=-1, keepdims=True) * (1.0 / LAT)
    spread = jnp.sum(centred * centred, axis=-1, keepdims=True)
    return centred * (lax.rsqrt(spread + LAT * 1e-5) * (0.5 * LAT ** 0.5))


def add_to(base, update):
    return (base.astype(F32) + update).astype(BF16)


def mm_features(feats, weight):
    return lax.dot_general(feats, weight, (((0,), (0,)), ((), ())), preferred_element_type=F32)


def embed_kernel(x_ref, w_in_ref, w_out_ref, o_ref):
    halves = [slice(s * ROWS, (s + 1) * ROWS) for s in range(SUB)]
    hid = [silu_twice(mm_features(0.5 * x_ref[:, cols], w_in_ref[0])) for cols in halves]
    upd = [mm(h, w_out_ref[0]) for h in hid]
    for s in range(SUB):
        o_ref[halves[s], :] = half_norm(upd[s]).astype(BF16)


def embed_static(feats, w_in, w_out, starts, name):
    depth, rows = feats.shape
    block = SUB * ROWS

    def kind(i):
        return sum((i >= s // block).astype(jnp.int32) for s in starts) if starts else 0

    return pl.pallas_call(
        embed_kernel,
        grid=(rows // block,),
        in_specs=[
            pl.BlockSpec((depth, block), lambda i: (0, i)),
            pl.BlockSpec((1, depth, LAT), lambda i: (kind(i), 0, 0)),
            pl.BlockSpec((1, LAT, LAT), lambda i: (kind(i), 0, 0)),
        ],
        out_specs=pl.BlockSpec((block, LAT), lambda i: (i, 0)),
        out_shape=jax.ShapeDtypeStruct((rows, LAT), BF16),
        compiler_params=pltpu.CompilerParams(vmem_limit_bytes=VMEM_LIMIT),
        cost_estimate=pl.CostEstimate(flops=6 * rows * LAT * LAT, bytes_accessed=2 * rows * LAT, transcendentals=0),
        name=name,
    )(feats, w_in, w_out)


def rows_of(sub, size):
    return pl.ds(sub * size, size)


LANE_COLS = [slice(c * LANES, (c + 1) * LANES) for c in range(LAT // LANES)]


def spread(buf, sub, cell_rows):
    for c, col in enumerate(LANE_COLS):
        for k in range(RATIO):
            buf[c, pl.ds(sub * ROWS + k, CELLS, stride=RATIO), :] = cell_rows[:, col]
    return jnp.concatenate([buf[c, rows_of(sub, ROWS), :] for c in range(len(LANE_COLS))], axis=1)


def gather_sum(buf, sub, node_rows):
    for c, col in enumerate(LANE_COLS):
        buf[c, rows_of(sub, ROWS), :] = node_rows[:, col]
    sums = []
    for c in range(len(LANE_COLS)):
        parts = [buf[c, pl.ds(sub * ROWS + k, CELLS, stride=RATIO), :] for k in range(RATIO)]
        sums.append(parts[0] + parts[1] + parts[2] + parts[3])
    return jnp.concatenate(sums, axis=1).astype(BF16)


FEAT_CUR = 88
FEAT_FORCE = 176
FEAT_ROWS = 192


def grid_kernel(names, decode, encode, *refs):
    r = dict(zip(names, refs))
    mean, std, diff_mean, diff_std = (r["stats"][:, i:i + 1] for i in range(4))
    subs = range(SUB)
    cols = [slice(s * ROWS, (s + 1) * ROWS) for s in subs]
    cur = [r["cur"][:, c] for c in cols]
    if decode:
        grid_cur = [r["grid_cur"][rows_of(s, ROWS), :] for s in subs]
        pre = []
        for s in subs:
            send = mm(r["h_in"][s, 0], r["wl"][LAT:2 * LAT, :])
            both = mm(r["m2g"][rows_of(s, ROWS), :], r["wl"][:LAT, :]) + mm(grid_cur[s], r["wl"][2 * LAT:, :])
            pre.append(both + spread(r["buf_send"], s, send))
        hid = [silu_twice(p) for p in pre]
        upd = [mm(h, r["wl_out"][...]) for h in hid]
        edge = [add_to(r["m2g"][rows_of(s, ROWS), :], half_norm(upd[s])) for s in subs]
        pre = [mm(grid_cur[s], r["wl_node"][:LAT, :]) + mm(edge[s], r["wl_node"][LAT:, :]) for s in subs]
        hid = [silu_twice(p) for p in pre]
        upd = [mm(h, r["wl_node_out"][...]) for h in hid]
        out = [add_to(grid_cur[s], half_norm(upd[s])) for s in subs]
        hid = [silu_twice(mm(o, r["w_hidden"][...])) for o in out]
        pred = [mm(h, r["w_final"][...]).T[:VARS] for h in hid]
        nxt = [cur[s] + diff_std * pred[s] + diff_mean for s in subs]
        for s in subs:
            r["next"][:, cols[s]] = nxt[s]
    if encode:
        if decode:
            first, second = cur, nxt
        else:
            first, second = [r["prev"][:, c] for c in cols], cur
        table = r["buf_feat"]
        feats = []
        for s in subs:
            table[VARS - 3:FEAT_CUR, cols[s]] = jnp.zeros((8, ROWS), F32)
            table[FEAT_FORCE - 8:FEAT_FORCE, cols[s]] = jnp.zeros((8, ROWS), F32)
            table[:VARS, cols[s]] = (first[s] - mean) / std
            table[FEAT_CUR:FEAT_CUR + VARS, cols[s]] = (second[s] - mean) / std
            table[FEAT_FORCE:, cols[s]] = r["force"][:, cols[s]]
            feats.append(0.5 * table[:, cols[s]].astype(BF16))
        hid = [silu_twice(mm_features(f, r["w_grid"][...])) for f in feats]
        v = [half_norm(mm(h, r["w_grid_out"][...])).astype(BF16) for h in hid]
        pre = []
        for s in subs:
            recv = mm(r["mesh"][rows_of(s, CELLS), :], r["wf"][2 * LAT:, :])
            both = mm(r["g2m"][rows_of(s, ROWS), :], r["wf"][:LAT, :]) + mm(v[s], r["wf"][LAT:2 * LAT, :])
            pre.append(both + spread(r["buf_recv"], s, recv))
        self_hid = [silu_twice(mm(x, r["w_self"][0])) for x in v]
        hid = [silu_twice(p) for p in pre]
        upd = [mm(h, r["wf_out"][...]) for h in hid]
        self_upd = [mm(h, r["w_self"][1]) for h in self_hid]
        total = [gather_sum(r["buf_sum"], s, add_to(r["g2m"][rows_of(s, ROWS), :], half_norm(upd[s])).astype(F32)) for s in subs]
        mesh = [r["mesh"][rows_of(s, CELLS), :] for s in subs]
        pre = [mm(mesh[s], r["wf_node"][:LAT, :]) + mm(total[s], r["wf_node"][LAT:, :]) for s in subs]
        for s in subs:
            r["grid_new"][rows_of(s, ROWS), :] = add_to(v[s], half_norm(self_upd[s]))
        hid = [silu_twice(p) for p in pre]
        upd = [mm(h, r["wf_node_out"][...]) for h in hid]
        for s in subs:
            r["h_out"][s, 0] = add_to(mesh[s], half_norm(upd[s]))


def grid_call(arrays, weights, decode, encode, name):
    tiles = arrays["cur"].shape[1] // ROWS
    lead = tiles // 2
    step_rows = SUB * ROWS
    node_spec = pl.BlockSpec((SUB, 1, CELLS, LAT), lambda i: (i % (lead // SUB), i // (lead // SUB), 0, 0))
    special = {
        "h_in": node_spec,
        "grid_cur": pl.BlockSpec((step_rows, LAT), lambda i: (i, 0)),
        "mesh": pl.BlockSpec((SUB * CELLS, LAT), lambda i: (i, 0)),
        "g2m": pl.BlockSpec((step_rows, LAT), lambda i: (i + 1, 0)),
        "m2g": pl.BlockSpec((step_rows, LAT), lambda i: (i + 1 + tiles // SUB, 0)),
    }
    names, specs, operands = [], [], []
    for key, arr in arrays.items():
        names.append(key)
        operands.append(arr)
        specs.append(special.get(key) or pl.BlockSpec((arr.shape[0], step_rows), lambda i: (0, i)))
    for key, arr in weights.items():
        names.append(key)
        operands.append(arr)
        specs.append(pl.BlockSpec(arr.shape, functools.partial(lambda nd, i: (0,) * nd, arr.ndim)))
    out_specs, out_shapes, scratch = [], [], []
    wide = pltpu.VMEM((len(LANE_COLS), step_rows, LANES), F32)
    if decode:
        names.append("next")
        out_specs.append(pl.BlockSpec((VARS, step_rows), lambda i: (0, i)))
        out_shapes.append(jax.ShapeDtypeStruct((VARS, tiles * ROWS), F32))
    if encode:
        names += ["grid_new", "h_out"]
        out_specs += [pl.BlockSpec((step_rows, LAT), lambda i: (i, 0)), node_spec]
        out_shapes += [jax.ShapeDtypeStruct((tiles * ROWS, LAT), BF16), jax.ShapeDtypeStruct((lead, 2, CELLS, LAT), BF16)]
    if decode:
        names.append("buf_send")
        scratch.append(wide)
    if encode:
        names += ["buf_recv", "buf_sum", "buf_feat"]
        scratch += [wide, wide, pltpu.VMEM((FEAT_ROWS, step_rows), F32)]
    return pl.pallas_call(
        functools.partial(grid_kernel, tuple(names), decode, encode),
        grid=(tiles // SUB,),
        in_specs=specs,
        out_specs=out_specs,
        out_shape=out_shapes,
        scratch_shapes=scratch,
        compiler_params=pltpu.CompilerParams(vmem_limit_bytes=VMEM_LIMIT),
        cost_estimate=pl.CostEstimate(flops=2 * 7 * tiles * ROWS * LAT * LAT * (decode + encode), bytes_accessed=2 ** 24, transcendentals=0),
        name=name,
    )(*operands)


def proc_kernel(first_edge, h_in, lat, w_ei, w_eo, w_ni, w_no, h_out, edge, mesh, proj, recv, total, turn, halo, b_ei, b_eo, b_ni, b_no, w_sem, e_sem, s_sem, r_sem):
    ring = 4
    me = lax.axis_index("gp")
    right = lax.rem(me + 1, ring)
    left = lax.rem(me + ring - 1, ring)

    def weight_copies(layer, slot):
        pairs = ((w_ei, b_ei), (w_eo, b_eo), (w_ni, b_ni), (w_no, b_no))
        return [pltpu.make_async_copy(src.at[layer], dst.at[slot], w_sem.at[slot, i]) for i, (src, dst) in enumerate(pairs)]

    edge_copies = [pltpu.make_async_copy(lat.at[pl.ds(first_edge + k * NODES, NODES)], edge.at[k], e_sem.at[k]) for k in range(OFFS)]
    for copy in weight_copies(1, 1) + edge_copies:
        copy.start()

    barrier = pltpu.get_barrier_semaphore()
    for peer in (left, right):
        pl.semaphore_signal(barrier, inc=1, device_id={"gp": peer}, device_id_type=pl.DeviceIdType.MESH)

    for c, col in enumerate(LANE_COLS):
        for q in range(Q):
            turn[c, pl.ds(q, RLOC, stride=Q), :] = h_in[q, :, col].astype(F32)
    for c, col in enumerate(LANE_COLS):
        mesh[:, col] = turn[c].astype(BF16)
    pl.semaphore_wait(barrier, 2)
    for copy in weight_copies(1, 1):
        copy.wait()

    def project(slot):
        for c in range(2):
            rows = pl.ds(c * 512, 512)
            nodes = mesh[rows, :]
            proj[pl.ds(8 + c * 512, 512), :] = mm(nodes, b_ei[slot, LAT:2 * LAT, :])
            recv[rows, :] = mm(nodes, b_ei[slot, 2 * LAT:, :])

    project(1)
    for copy in edge_copies:
        copy.wait()

    def edge_tile(slot, t):
        start = pl.multiple_of(t * TILE, TILE)
        rows = pl.ds(start, TILE)
        at_recv = recv[rows, :]
        here = proj[pl.ds(start + 8, TILE), :].reshape(TILE // Q, Q, LAT)

        def sender(k):
            if k == 0:
                return proj[pl.ds(start + 16, TILE), :]
            if k == 1:
                return proj[rows, :]
            shift = {2: Q - 1, 3: 1, 4: Q - 2, 5: 2}[k]
            return pltpu.roll(here, shift, 1).reshape(TILE, LAT)

        w_first = b_ei[slot, :LAT, :]
        w_second = b_eo[slot]
        chunks = OFFS * TILE // CHUNK
        per = CHUNK // TILE
        old, hid, upd = {}, {}, {}
        acc = [None]

        def stage_a(c):
            pair = edge[per * c:per * c + per, rows, :].reshape(CHUNK, LAT)
            old[c] = pair
            terms = jnp.concatenate([sender(per * c + j) + at_recv for j in range(per)], axis=0)
            hid[c] = silu_twice(mm(pair, w_first) + terms)

        def stage_b(c):
            upd[c] = mm(hid[c], w_second)

        def stage_c(c):
            new = add_to(old[c], half_norm(upd[c]))
            edge[per * c:per * c + per, rows, :] = new.reshape(per, TILE, LAT)
            wide = new.astype(F32)
            for j in range(per):
                part = wide[j * TILE:(j + 1) * TILE]
                acc[0] = part if acc[0] is None else acc[0] + part

        for c in range(chunks + LAG_C):
            if c < chunks:
                stage_a(c)
            if LAG_B <= c < chunks + LAG_B:
                stage_b(c - LAG_B)
            if LAG_C <= c:
                stage_c(c - LAG_C)
        total[rows, :] = acc[0].astype(BF16)

    def update_nodes(slot, last):
        chunks = [pl.ds(c * 512, 512) for c in range(2)]
        nodes = [mesh[rows, :] for rows in chunks]
        hid = [silu_twice(mm(nodes[c], b_ni[slot, :LAT, :]) + mm(total[chunks[c], :], b_ni[slot, LAT:, :])) for c in range(2)]
        upd = [mm(h, b_no[slot]) for h in hid]
        for c in range(2):
            new = add_to(nodes[c], half_norm(upd[c]))
            if last:
                for d, col in enumerate(LANE_COLS):
                    turn[d, chunks[c], :] = new[:, col].astype(F32)
            else:
                mesh[chunks[c], :] = new
                proj[pl.ds(8 + c * 512, 512), :] = mm(new, b_ei[1 - slot, LAT:2 * LAT, :])
                recv[chunks[c], :] = mm(new, b_ei[1 - slot, 2 * LAT:, :])

    def layer(l, last):
        slot = lax.rem(l, 2)
        if not last:
            for copy in weight_copies(l + 1, 1 - slot):
                copy.start()
        sends = [
            pltpu.make_async_remote_copy(
                src_ref=proj.at[pl.ds(first, 8)],
                dst_ref=halo.at[slot, side],
                send_sem=s_sem.at[side],
                recv_sem=r_sem.at[slot, side],
                device_id={"gp": peer},
                device_id_type=pl.DeviceIdType.MESH)
            for side, first, peer in ((0, NODES, right), (1, 8, left))]
        for send in sends:
            send.start()

        def pair(base):
            def body(i, carry):
                edge_tile(slot, lax.rem(i + base, NODES // TILE))
                return carry
            lax.fori_loop(0, 2, body, 0)

        pair(1)
        for send in sends:
            send.wait_recv()
        below = halo[slot, 0]
        above = halo[slot, 1]
        proj[0:8, :] = jnp.where(me == 0, pltpu.roll(below, 1, 0), below)
        proj[8 + NODES:16 + NODES, :] = jnp.where(me == ring - 1, pltpu.roll(above, Q - 1, 0), above)
        pair(3)
        for send in sends:
            send.wait_send()
        if not last:
            for copy in weight_copies(l + 1, 1 - slot):
                copy.wait()
        update_nodes(slot, last)

    def loop_body(l, carry):
        layer(l, False)
        return carry

    lax.fori_loop(1, LAYERS, loop_body, 0)
    layer(jnp.int32(LAYERS), True)
    for c, col in enumerate(LANE_COLS):
        for q in range(Q):
            h_out[q, :, col] = turn[c, pl.ds(q, RLOC, stride=Q), :].astype(BF16)


def processor(h_in, lat, first_edge, w_edge_in, w_edge_out, w_node_in, w_node_out):
    hbm = pl.BlockSpec(memory_space=pl.ANY)
    vmem = pl.BlockSpec(memory_space=pltpu.VMEM)
    rows = NODES * (OFFS * 2 + 8)
    return pl.pallas_call(
        functools.partial(proc_kernel, first_edge),
        in_specs=[vmem, hbm, hbm, hbm, hbm, hbm],
        out_specs=vmem,
        out_shape=jax.ShapeDtypeStruct((Q, RLOC, LAT), BF16),
        scratch_shapes=[
            pltpu.VMEM((OFFS, NODES, LAT), BF16),
            pltpu.VMEM((NODES, LAT), BF16),
            pltpu.VMEM((NODES + 16, LAT), F32),
            pltpu.VMEM((NODES, LAT), F32),
            pltpu.VMEM((NODES, LAT), BF16),
            pltpu.VMEM((LAT // LANES, NODES, LANES), F32),
            pltpu.VMEM((2, 2, 8, LAT), F32),
            pltpu.VMEM((2, 3 * LAT, LAT), BF16),
            pltpu.VMEM((2, LAT, LAT), BF16),
            pltpu.VMEM((2, 2 * LAT, LAT), BF16),
            pltpu.VMEM((2, LAT, LAT), BF16),
            pltpu.SemaphoreType.DMA((2, 4)),
            pltpu.SemaphoreType.DMA((OFFS,)),
            pltpu.SemaphoreType.DMA((2,)),
            pltpu.SemaphoreType.DMA((2, 2)),
        ],
        compiler_params=pltpu.CompilerParams(collective_id=0, has_side_effects=True, vmem_limit_bytes=VMEM_LIMIT),
        cost_estimate=pl.CostEstimate(flops=2 * LAYERS * rows * LAT * LAT, bytes_accessed=60 * 2 ** 20, transcendentals=0),
        name="processor",
    )(h_in, lat, w_edge_in, w_edge_out, w_node_in, w_node_out)


def solution(mesh):
    ring = mesh.shape["gp"]
    row_spec = P(("dp", "gp"))
    edge_spec = P(("dp", "gp"), None, None)
    whole = P()

    def exchange(x):
        return lax.all_to_all(x, "gp", 0, 0)

    def local_run(x_prev, x_cur, forcing, grid_static, g2m_feat, m2g_feat, mesh_feat, mesh_edge_feat, norm_stats, w_grid_in, w_mesh_in, w_eemb_in, w_embed_out, w_edge_in, w_edge_out, w_node_in, w_node_out, w_grid_self, w_out_hidden, w_out_final):
        grid_dev = x_prev.shape[0]
        mesh_dev = mesh_feat.shape[0]
        half = mesh_dev // 2
        deep = 8

        def padded(x):
            return jnp.pad(x, ((0, deep - x.shape[0]), (0, 0)))

        edges = mesh_edge_feat.astype(BF16).transpose(1, 2, 0).reshape(OFFS * 4, 2, ring, RLOC).transpose(2, 0, 1, 3)
        edges = exchange(edges)
        edges = edges.reshape(ring, OFFS, 4, 2, RLOC).transpose(2, 1, 4, 0, 3).reshape(4, OFFS * RLOC, Q)
        edges = padded(jnp.roll(edges, -1, axis=2).reshape(4, OFFS * NODES))
        node_rows = mesh_feat.astype(BF16).T
        g2m_rows = g2m_feat.astype(BF16).T
        head = jnp.concatenate([node_rows[:, :half]] + [g2m_rows[:, k * half:(k + 1) * half] for k in range(RATIO)], axis=0)
        head = lax.ppermute(head, "gp", [(s, (s - 1) % ring) for s in range(ring)])
        node_rows = padded(jnp.concatenate([node_rows[:, half:], head[:3]], axis=1))
        g2m_rows = padded(jnp.concatenate([g2m_rows[:, RATIO * half:]] + [head[3 + 4 * k:7 + 4 * k] for k in range(RATIO)], axis=1))
        feats = jnp.concatenate([node_rows, g2m_rows, padded(m2g_feat.astype(BF16).T)], axis=1)
        lat = embed_static(feats, jnp.stack([padded(w_mesh_in), padded(w_eemb_in[0]), padded(w_eemb_in[1])]), w_embed_out[1:4], (mesh_dev, mesh_dev + grid_dev), "embed")
        edge_lat = embed_static(edges, padded(w_eemb_in[2])[None], w_embed_out[4:5], (), "embed_edges")

        w_grid = jnp.concatenate([
            jnp.pad(w_grid_in[:VARS], ((0, FEAT_CUR - VARS), (0, 0))),
            jnp.pad(w_grid_in[VARS:2 * VARS], ((0, FEAT_CUR - VARS), (0, 0))),
            padded(w_grid_in[2 * VARS:2 * VARS + 5]), padded(w_grid_in[2 * VARS + 5:])], axis=0)
        w_final = jnp.pad(w_out_final, ((0, 0), (0, LANES - VARS)))
        last = w_edge_in.shape[0] - 1
        stats = norm_stats.T
        enc_w = {"stats": stats, "w_grid": w_grid, "w_grid_out": w_embed_out[0], "wf": w_edge_in[0], "wf_out": w_edge_out[0], "wf_node": w_node_in[0], "wf_node_out": w_node_out[0], "w_self": w_grid_self}
        dec_w = {"stats": stats, "wl": w_edge_in[last], "wl_out": w_edge_out[last], "wl_node": w_node_in[last], "wl_node_out": w_node_out[last], "w_hidden": w_out_hidden, "w_final": w_final}
        static_rows = padded(grid_static.T)
        force = [jnp.concatenate([padded(forcing[:, s, :].T), static_rows], axis=0) for s in range(2)]

        def process(h):
            h = exchange(h).reshape(Q, RLOC, LAT)
            h = processor(h, edge_lat, 0, w_edge_in, w_edge_out, w_node_in, w_node_out)
            return exchange(h.reshape(ring, 2, RLOC, LAT))

        now = x_cur.T
        grid_lat, h = grid_call({"cur": now, "prev": x_prev.T, "force": force[0], "g2m": lat, "mesh": lat}, enc_w, False, True, "encode")
        h = process(h)
        x_next, grid_lat, h = grid_call({"cur": now, "h_in": h, "grid_cur": grid_lat, "m2g": lat, "force": force[1], "g2m": lat, "mesh": lat}, {**dec_w, **enc_w}, True, True, "decode_encode")
        h = process(h)
        x_after, = grid_call({"cur": x_next, "h_in": h, "grid_cur": grid_lat, "m2g": lat}, dec_w, True, False, "decode")
        return x_next.T, x_after.T

    in_specs = (row_spec, row_spec, edge_spec, row_spec, row_spec, row_spec, row_spec, edge_spec, whole) + (whole,) * 11
    return jax.shard_map(local_run, mesh=mesh, in_specs=in_specs, out_specs=(row_spec, row_spec), check_vma=False)
```

profile of v0, /device:TPU:0, one launch (start us, length us, event | category | flops | bytes accessed | tf_op | source)
XLA Modules:
  0.0 555.4 jit_solution(1612283662311417352)
XLA Ops:
  0.6 0.7 convert_bitcast_fusion.3
  1.4 0.9 convert_bitcast_fusion.2
  2.2 0.2 concatenate.26
  2.5 2.8 collective-permute-start
  5.3 0.9 convert_bitcast_fusion
  6.2 0.6 copy.47
  6.9 3.3 all-to-all-start.1
  10.2 0.8 fusion.18
  11.0 0.9 slice.122
  11.9 0.7 pad_bitcast_fusion.3
  12.6 0.7 slice_bitcast_fusion.9
  13.3 0.9 convert_bitcast_fusion.1
  14.1 1.0 slice_select_fusion
  15.1 1.1 fusion.19
  16.3 2.2 fusion.17
  18.5 3.0 slice_bitcast_fusion.2
  21.5 3.9 slice_bitcast_fusion
  25.4 0.1 copy_bitcast_fusion
  25.5 0.0 copy-start.5
  25.5 3.0 slice_bitcast_fusion.4
  28.6 0.6 pad_maximum_fusion.1.w_in_ref
  29.2 0.9 select_maximum_fusion
  30.0 0.7 fusion.10.refs_6_.refs_14_
  30.7 0.6 pad_bitcast_fusion.w_in_ref
  31.3 1.3 slice.120.w_out_ref
  32.6 0.7 copy.46
  33.4 0.7 fusion.13.x_ref
  34.1 13.4 %embed.1.refs_3_.refs_4_.refs_5_.refs_6_ = bf16[9216,512]{1,0:T(8,128)(2,1)} custom-call(bf16[8,9216]{1,0:T(8,128)(2,1)} %fusion.13.x_ref, bf16[3,8,512]{2,1,0:T(8,128)(2,1)} %pad_maximum_fusion.1.w_in_ref, bf16[3,512,512]{2,1,0:T(8,128)(2,1)} %slice.120.w_out_ref), custom_call_target="tpu_custom_call" | custom-call | flops 14495514624 | bytes 9437184 | tf_op jit(solution)/shard_map/embed/pallas_call | solution.py:68
  47.5 26.1 %encode.1 = (bf16[4096,512]{1,0:T(8,128)(2,1)}, bf16[4,2,128,512]{3,2,1,0:T(8,128)(2,1)}) custom-call(f32[83,4096]{1,0:T(8,128)} %bitcast.75, f32[83,4096]{1,0:T(8,128)} %bitcast.74, f32[16,4096]{1,0:T(8,128)} %get-tuple-element.27.refs_2_, bf16[9216,512]{1,0:T(8,128)(2,1)} %embed.1.refs_3_.refs_4_.refs_5_.refs_6_, ...), custom_call_target="tpu_custom_call" | custom-call | flops 15032385536 | bytes 16777216 | tf_op jit(solution)/shard_map/encode/pallas_call | solution.py:211
  73.6 3.7 all-to-all-start
  77.3 0.1 reshape.31
  77.5 0.4 copy.50
  77.9 0.9 reshape.32
  78.8 0.7 pad.69.x_ref
  79.5 9.4 %embed_edges.1.lat = bf16[6144,512]{1,0:T(8,128)(2,1)} custom-call(bf16[8,6144]{1,0:T(8,128)(2,1)} %pad.69.x_ref, bf16[1,8,512]{2,1,0:T(8,128)(2,1)} %pad_bitcast_fusion.w_in_ref, bf16[1,512,512]{2,1,0:T(8,128)(2,1)} %get-tuple-element.20.w_out_ref), custom_call_target="tpu_custom_call" | custom-call | flops 9663676416 | bytes 6291456 | tf_op jit(solution)/shard_map/embed_edges/pallas_call | solution.py:68
  88.9 2.6 all-to-all-done
  91.5 1.0 copy-done.1
  92.4 168.5 %processor.2 = bf16[8,128,512]{2,1,0:T(8,128)(2,1)} custom-call(bf16[8,128,512]{2,1,0:T(8,128)(2,1)} %bitcast.64, bf16[6144,512]{1,0:T(8,128)(2,1)} %embed_edges.1.lat, bf16[14,1536,512]{2,1,0:T(8,128)(2,1)} %w_ei.3, bf16[14,512,512]{2,1,0:T(8,128)(2,1)} %w_eo.3, bf16[14,1024,512]{2,1,0:T(8,128)(2,1)} %w_ni.3, bf16[14,512,512]{2,1,0:T(8,128)(2,1)} %w_no.3), custom_call_target="tpu_custom_call" | custom-call | flops 128849018880 | bytes 62914560 | tf_op jit(solution)/shard_map/processor/pallas_call | solution.py:377
  260.9 3.9 all-to-all-start.2
  264.9 0.1 copy.52
  265.0 0.7 pad.72.refs_13_.refs_10_
  265.7 13.3 %all-to-all-done.2.refs_1_ = bf16[4,2,128,512]{3,2,1,0:T(8,128)(2,1)S(1)} async-done(((bf16[4,2,128,512]{3,2,1,0:T(8,128)(2,1)}), bf16[4,2,128,512]{3,2,1,0:T(8,128)(2,1)S(1)}, u32[]{:S(2)}, u32[]{:S(2)}) %all-to-all-start.2) | async-done | bytes 1048608 | tf_op jit(solution)/shard_map/all_to_all | solution.py:412
  279.0 1.0 copy-done.2
  280.1 46.5 %decode_encode.1 = (f32[83,4096]{1,0:T(8,128)}, bf16[4096,512]{1,0:T(8,128)(2,1)}, bf16[4,2,128,512]{3,2,1,0:T(8,128)(2,1)}) custom-call(f32[83,4096]{1,0:T(8,128)} %bitcast.76, bf16[4,2,128,512]{3,2,1,0:T(8,128)(2,1)} %copy-done.2, bf16[4096,512]{1,0:T(8,128)(2,1)} %get-tuple-element.8.refs_2_, bf16[9216,512]{1,0:T(8,128)(2,1)} %embed.1.refs_3_.refs_4_.refs_5_.refs_6_, ...), custom_call_target="tpu_custom_call" | custom-call | flops 30064771072 | bytes 16777216 | tf_op jit(solution)/shard_map/decode_encode/pallas_call | solution.py:211
  326.5 18.6 %all_to_all.25 = bf16[4,2,128,512]{3,2,1,0:T(8,128)(2,1)} all-to-all(bf16[4,2,128,512]{3,2,1,0:T(8,128)(2,1)} %get-tuple-element.10), channel_id=1, replica_groups=mesh['dp'=2,'gp'=4] {'gp'}, dimensions={0} | all-to-all | bytes 2097152 | tf_op jit(solution)/shard_map/all_to_all | solution.py:412
  345.2 168.4 %processor.3 = bf16[8,128,512]{2,1,0:T(8,128)(2,1)} custom-call(bf16[8,128,512]{2,1,0:T(8,128)(2,1)} %bitcast.66, bf16[6144,512]{1,0:T(8,128)(2,1)} %embed_edges.1.lat, bf16[14,1536,512]{2,1,0:T(8,128)(2,1)} %w_ei.3, bf16[14,512,512]{2,1,0:T(8,128)(2,1)} %w_eo.3, bf16[14,1024,512]{2,1,0:T(8,128)(2,1)} %w_ni.3, bf16[14,512,512]{2,1,0:T(8,128)(2,1)} %w_no.3), custom_call_target="tpu_custom_call" | custom-call | flops 128849018880 | bytes 62914560 | tf_op jit(solution)/shard_map/processor/pallas_call | solution.py:377
  513.6 18.4 %all_to_all.26.refs_1_ = bf16[4,2,128,512]{3,2,1,0:T(8,128)(2,1)} all-to-all(bf16[4,2,128,512]{3,2,1,0:T(8,128)(2,1)} %bitcast.67), channel_id=1, replica_groups=mesh['dp'=2,'gp'=4] {'gp'}, dimensions={0} | all-to-all | bytes 2097152 | tf_op jit(solution)/shard_map/all_to_all | solution.py:412
  532.0 23.2 %decode.1 = f32[83,4096]{1,0:T(8,128)} custom-call(f32[83,4096]{1,0:T(8,128)} %get-tuple-element.9.refs_0_, bf16[4,2,128,512]{3,2,1,0:T(8,128)(2,1)} %all_to_all.26.refs_1_, bf16[4096,512]{1,0:T(8,128)(2,1)} %get-tuple-element.11.refs_2_, bf16[9216,512]{1,0:T(8,128)(2,1)} %embed.1.refs_3_.refs_4_.refs_5_.refs_6_, f32[83,4]{1,0:T(8,128)} %bitcast.73, ...), custom_call_target="tpu_custom_call" | custom-call | flops 15032385536 | bytes 16777216 | tf_op jit(solution)/shard_map/decode/pallas_call | solution.py:211
  (27 shorter events, 0.2 us)
Async XLA Ops:
  2.5 30.8 %collective-permute-start = (bf16[19,512]{1,0:T(8,128)(2,1)S(1)}, bf16[19,512]{1,0:T(8,128)(2,1)S(1)}, u32[]{:S(2)}, u32[]{:S(2)}) collective-permute-start(bf16[19,512]{1,0:T(8,128)(2,1)S(1)} %concatenate.26), channel_id=1, source_target_pairs={{0,3},{1,0},{2,1},{3,2},{4,7},{5,4},{6,5},{7,6}} | collective-permute-start | bytes 58376 | tf_op jit(solution)/shard_map/ppermute | solution.py:430
  6.9 66.7 %all-to-all-start.1 = ((bf16[4,24,2,128]{3,2,1,0:T(2,128)(2,1)}), bf16[4,24,2,128]{3,2,1,0:T(2,128)(2,1)S(1)}, u32[]{:S(2)}, u32[]{:S(2)}) async-start(bf16[4,24,2,128]{3,2,1,0:T(2,128)(2,1)} %copy.47), calls=%async_computation.1 | async-start | bytes 98304 | tf_op jit(solution)/shard_map/all_to_all | solution.py:412
  21.5 7.6 %copy-start.3 = (f32[4096,5]{0,1:T(8,128)S(1)}, f32[4096,5]{0,1:T(8,128)}, u32[]{:S(2)}) copy-start(f32[4096,5]{0,1:T(8,128)} %param.23) | copy-start | bytes 245764
  25.4 5.9 %copy-start = (bf16[5,512,512]{2,1,0:T(8,128)(2,1)S(1)}, bf16[5,512,512]{2,1,0:T(8,128)(2,1)}, u32[]{:S(2)}) copy-start(bf16[5,512,512]{2,1,0:T(8,128)(2,1)} %param.32) | copy-start | bytes 7864324
  25.5 7.0 %copy-start.5 = (f32[4,83]{1,0:T(4,128)S(1)}, f32[4,83]{1,0:T(4,128)}, u32[]{:S(2)}) copy-start(f32[4,83]{1,0:T(4,128)} %param.28) | copy-start | bytes 3988
  73.6 17.9 %all-to-all-start = ((bf16[4,2,128,512]{3,2,1,0:T(8,128)(2,1)}), bf16[4,2,128,512]{3,2,1,0:T(8,128)(2,1)S(1)}, u32[]{:S(2)}, u32[]{:S(2)}) async-start(bf16[4,2,128,512]{3,2,1,0:T(8,128)(2,1)} %get-tuple-element.7), calls=%async_computation | async-start | bytes 2097152 | tf_op jit(solution)/shard_map/all_to_all | solution.py:412
  91.5 1.0 copy-start.1
  92.4 172.4 %copy-start.4 = (bf16[512,83]{0,1:T(8,128)(2,1)S(1)}, bf16[512,83]{0,1:T(8,128)(2,1)}, u32[]{:S(2)}) copy-start(bf16[512,83]{0,1:T(8,128)(2,1)} %param.39) | copy-start | bytes 254980
  260.9 18.1 %all-to-all-start.2 = ((bf16[4,2,128,512]{3,2,1,0:T(8,128)(2,1)}), bf16[4,2,128,512]{3,2,1,0:T(8,128)(2,1)S(1)}, u32[]{:S(2)}, u32[]{:S(2)}) async-start(bf16[4,2,128,512]{3,2,1,0:T(8,128)(2,1)} %bitcast.65), calls=%async_computation.2 | async-start | bytes 2097152 | tf_op jit(solution)/shard_map/all_to_all | solution.py:412
  279.0 1.0 copy-start.2
where the time goes:
time: 562 us; the launch traced here: 555 us
  Pallas kernels  456 us (81%)
  blocking collectives  37 us (7%)
  local copies, waits for them, and re-layouts  25 us (4%)
  waiting for transfers between devices  15.9 us (3%)
  starting transfers between devices  13.7 us (2%)
  other arithmetic  7.19 us (1%)
    pallas_call x2, Pallas kernels, processor(): pl.pallas_call(functools.partial(proc_kernel, first_edge), in_specs=[vmem...  337 us
    pallas_call x3, Pallas kernels, grid_call(): pl.pallas_call(functools.partial(grid_kernel, tuple(names), decode, encod...  95.8 us
    all_to_all x2, blocking collectives, exchange(): return lax.all_to_all(x, 'gp', 0, 0)  37 us
    pallas_call x2, Pallas kernels, embed_static(): pl.pallas_call(embed_kernel, grid=(rows // block,), in_specs=[pl.BlockSpe...  22.9 us
    all_to_all x3, waiting for transfers between devices, exchange(): return lax.all_to_all(x, 'gp', 0, 0)  15.9 us
  transfers between devices with their start and end apart: 4, of which 2 were waited for; matrix products, arithmetic and copies ran while one was open for 5% of the time, Pallas kernels for 9%

commit v1 on v0

--- a/solution.py
+++ b/solution.py
@@ -23,8 +23,6 @@
 LAYERS = 12
 TILE = 256
 CHUNK = 512
-LAG_B = 1
-LAG_C = 2
 VMEM_LIMIT = 60 * 1024 * 1024
 
 
@@ -58,7 +56,7 @@
         o_ref[halves[s], :] = half_norm(upd[s]).astype(BF16)
 
 
-def embed_static(feats, w_in, w_out, starts, name):
+def embed_static(feats, w_in, w_out, first, starts, name):
     depth, rows = feats.shape
     block = SUB * ROWS
 
@@ -71,7 +69,7 @@
         in_specs=[
             pl.BlockSpec((depth, block), lambda i: (0, i)),
             pl.BlockSpec((1, depth, LAT), lambda i: (kind(i), 0, 0)),
-            pl.BlockSpec((1, LAT, LAT), lambda i: (kind(i), 0, 0)),
+            pl.BlockSpec((1, LAT, LAT), lambda i: (kind(i) + first, 0, 0)),
         ],
         out_specs=pl.BlockSpec((block, LAT), lambda i: (i, 0)),
         out_shape=jax.ShapeDtypeStruct((rows, LAT), BF16),
@@ -79,6 +77,44 @@
         cost_estimate=pl.CostEstimate(flops=6 * rows * LAT * LAT, bytes_accessed=2 * rows * LAT, transcendentals=0),
         name=name,
     )(feats, w_in, w_out)
+
+
+RING = 4
+
+
+def greet():
+    me = lax.axis_index("gp")
+    barrier = pltpu.get_barrier_semaphore()
+    for hop in range(1, RING):
+        pl.semaphore_signal(barrier, inc=1, device_id={"gp": lax.rem(me + hop, RING)}, device_id_type=pl.DeviceIdType.MESH)
+
+
+def greeted():
+    pl.semaphore_wait(pltpu.get_barrier_semaphore(), RING - 1)
+
+
+class Parcel:
+
+    def __init__(self, peer, src, dst, send_sem, recv_sem):
+        self.peer, self.src, self.dst, self.send_sem, self.recv_sem = peer, src, dst, send_sem, recv_sem
+
+    def remote(self):
+        return pltpu.make_async_remote_copy(src_ref=self.src, dst_ref=self.dst, send_sem=self.send_sem, recv_sem=self.recv_sem, device_id={"gp": self.peer}, device_id_type=pl.DeviceIdType.MESH)
+
+    def either(self, remote_act, local_act):
+        me = lax.axis_index("gp")
+        pl.when(self.peer != me)(lambda: getattr(self.remote(), remote_act)())
+        if local_act:
+            pl.when(self.peer == me)(lambda: getattr(pltpu.make_async_copy(self.src, self.dst, self.send_sem), local_act)())
+
+    def start(self):
+        self.either("start", "start")
+
+    def wait_sent(self):
+        self.either("wait_send", "wait")
+
+    def wait_arrived(self):
+        self.either("wait_recv", None)
 
 
 def rows_of(sub, size):
@@ -167,8 +203,30 @@
             r["grid_new"][rows_of(s, ROWS), :] = add_to(v[s], half_norm(self_upd[s]))
         hid = [silu_twice(p) for p in pre]
         upd = [mm(h, r["wf_node_out"][...]) for h in hid]
-        for s in subs:
-            r["h_out"][s, 0] = add_to(mesh[s], half_norm(upd[s]))
+        step = pl.program_id(0)
+        me = lax.axis_index("gp")
+
+        def parcel(tile):
+            slot = 2 * me + tile // RING
+            return Parcel(tile % RING, r["h_buf"].at[tile], r["h_out"].at[slot], r["send_sem"].at[tile], r["recv_sem"].at[slot])
+
+        for s in subs:
+            r["h_buf"][step * SUB + s] = add_to(mesh[s], half_norm(upd[s]))
+
+        @pl.when(step == 0)
+        def first_step():
+            greet()
+            greeted()
+
+        for s in subs:
+            parcel(step * SUB + s).start()
+
+        @pl.when(step == pl.num_programs(0) - 1)
+        def last_step():
+            for tile in range(2 * RING):
+                parcel(tile).wait_sent()
+            for slot in range(2 * RING):
+                Parcel(slot // 2, r["h_buf"].at[slot], r["h_out"].at[slot], r["send_sem"].at[slot], r["recv_sem"].at[slot]).wait_arrived()
 
 
 def grid_call(arrays, weights, decode, encode, name):
@@ -190,8 +248,12 @@
         specs.append(special.get(key) or pl.BlockSpec((arr.shape[0], step_rows), lambda i: (0, i)))
     for key, arr in weights.items():
         names.append(key)
+        if isinstance(arr, tuple):
+            arr, layer = arr
+            specs.append(pl.BlockSpec((None,) + arr.shape[1:], functools.partial(lambda at, nd, i: (at,) + (0,) * nd, layer, arr.ndim - 1)))
+        else:
+            specs.append(pl.BlockSpec(arr.shape, functools.partial(lambda nd, i: (0,) * nd, arr.ndim)))
         operands.append(arr)
-        specs.append(pl.BlockSpec(arr.shape, functools.partial(lambda nd, i: (0,) * nd, arr.ndim)))
     out_specs, out_shapes, scratch = [], [], []
     wide = pltpu.VMEM((len(LANE_COLS), step_rows, LANES), F32)
     if decode:
@@ -200,14 +262,16 @@
         out_shapes.append(jax.ShapeDtypeStruct((VARS, tiles * ROWS), F32))
     if encode:
         names += ["grid_new", "h_out"]
-        out_specs += [pl.BlockSpec((step_rows, LAT), lambda i: (i, 0)), node_spec]
-        out_shapes += [jax.ShapeDtypeStruct((tiles * ROWS, LAT), BF16), jax.ShapeDtypeStruct((lead, 2, CELLS, LAT), BF16)]
+        out_specs += [pl.BlockSpec((step_rows, LAT), lambda i: (i, 0)), pl.BlockSpec(memory_space=pltpu.HBM)]
+        out_shapes += [jax.ShapeDtypeStruct((tiles * ROWS, LAT), BF16), jax.ShapeDtypeStruct((Q, RLOC, LAT), BF16)]
     if decode:
         names.append("buf_send")
         scratch.append(wide)
     if encode:
-        names += ["buf_recv", "buf_sum", "buf_feat"]
-        scratch += [wide, wide, pltpu.VMEM((FEAT_ROWS, step_rows), F32)]
+        names += ["buf_recv", "buf_sum", "buf_feat", "h_buf", "send_sem", "recv_sem"]
+        scratch += [wide, wide, pltpu.VMEM((FEAT_ROWS, step_rows), F32), pltpu.VMEM((tiles, CELLS, LAT), BF16)]
+        scratch += [pltpu.SemaphoreType.DMA((tiles,))] * 2
+    params = dict(collective_id=1 + decode, has_side_effects=True) if encode else {}
     return pl.pallas_call(
         functools.partial(grid_kernel, tuple(names), decode, encode),
         grid=(tiles // SUB,),
@@ -215,61 +279,77 @@
         out_specs=out_specs,
         out_shape=out_shapes,
         scratch_shapes=scratch,
-        compiler_params=pltpu.CompilerParams(vmem_limit_bytes=VMEM_LIMIT),
+        compiler_params=pltpu.CompilerParams(vmem_limit_bytes=VMEM_LIMIT, **params),
         cost_estimate=pl.CostEstimate(flops=2 * 7 * tiles * ROWS * LAT * LAT * (decode + encode), bytes_accessed=2 ** 24, transcendentals=0),
         name=name,
     )(*operands)
 
 
-def proc_kernel(first_edge, h_in, lat, w_ei, w_eo, w_ni, w_no, h_out, edge, mesh, proj, recv, total, turn, halo, b_ei, b_eo, b_ni, b_no, w_sem, e_sem, s_sem, r_sem):
-    ring = 4
+def proc_kernel(first_edge, h_in, lat, w_ei, w_eo, w_ni, w_no, h_out, edge, mesh, proj, recv, total, turn, out_buf, halo, b_ei, b_eo, b_ni, b_no, w_sem, e_sem, s_sem, r_sem, o_send, o_recv):
     me = lax.axis_index("gp")
-    right = lax.rem(me + 1, ring)
-    left = lax.rem(me + ring - 1, ring)
-
-    def weight_copies(layer, slot):
-        pairs = ((w_ei, b_ei), (w_eo, b_eo), (w_ni, b_ni), (w_no, b_no))
-        return [pltpu.make_async_copy(src.at[layer], dst.at[slot], w_sem.at[slot, i]) for i, (src, dst) in enumerate(pairs)]
+    right = lax.rem(me + 1, RING)
+    left = lax.rem(me + RING - 1, RING)
+
+    def edge_weights(layer):
+        slot = lax.rem(layer, 2)
+        return [pltpu.make_async_copy(src.at[layer], dst.at[slot], w_sem.at[slot, i]) for i, (src, dst) in enumerate(((w_ei, b_ei), (w_eo, b_eo)))]
+
+    def node_weights(layer):
+        slot = lax.rem(layer, 2)
+        return [pltpu.make_async_copy(src.at[layer], dst.at[slot], w_sem.at[slot, 2 + i]) for i, (src, dst) in enumerate(((w_ni, b_ni), (w_no, b_no)))]
+
+    def start_all(copies):
+        for copy in copies:
+            copy.start()
+
+    def wait_all(copies):
+        for copy in copies:
+            copy.wait()
 
     edge_copies = [pltpu.make_async_copy(lat.at[pl.ds(first_edge + k * NODES, NODES)], edge.at[k], e_sem.at[k]) for k in range(OFFS)]
-    for copy in weight_copies(1, 1) + edge_copies:
-        copy.start()
-
-    barrier = pltpu.get_barrier_semaphore()
-    for peer in (left, right):
-        pl.semaphore_signal(barrier, inc=1, device_id={"gp": peer}, device_id_type=pl.DeviceIdType.MESH)
-
+    start_all(edge_weights(1) + node_weights(1) + edge_copies)
+
+    greet()
     for c, col in enumerate(LANE_COLS):
         for q in range(Q):
             turn[c, pl.ds(q, RLOC, stride=Q), :] = h_in[q, :, col].astype(F32)
     for c, col in enumerate(LANE_COLS):
         mesh[:, col] = turn[c].astype(BF16)
-    pl.semaphore_wait(barrier, 2)
-    for copy in weight_copies(1, 1):
-        copy.wait()
-
-    def project(slot):
-        for c in range(2):
-            rows = pl.ds(c * 512, 512)
-            nodes = mesh[rows, :]
-            proj[pl.ds(8 + c * 512, 512), :] = mm(nodes, b_ei[slot, LAT:2 * LAT, :])
-            recv[rows, :] = mm(nodes, b_ei[slot, 2 * LAT:, :])
-
-    project(1)
-    for copy in edge_copies:
-        copy.wait()
-
-    def edge_tile(slot, t):
-        start = pl.multiple_of(t * TILE, TILE)
+    greeted()
+    wait_all(edge_weights(1) + node_weights(1))
+    total[...] = jnp.zeros_like(total)
+    for c in range(2):
+        rows = pl.ds(c * 512, 512)
+        proj[1, pl.ds(8 + c * 512, 512), :] = mm(mesh[rows, :], b_ei[1, LAT:2 * LAT, :])
+        recv[1, rows, :] = mm(mesh[rows, :], b_ei[1, 2 * LAT:, :])
+    wait_all(edge_copies)
+
+    def order(j):
+        return lax.rem(j + 1, 3) + 2 * (j // 3)
+
+    def node_rows(t):
+        return pl.ds(pl.multiple_of(t * TILE, TILE), TILE)
+
+    def tile_step(l, j):
+        slot = lax.rem(l, 2)
+        start = pl.multiple_of(order(j) * TILE, TILE)
         rows = pl.ds(start, TILE)
-        at_recv = recv[rows, :]
-        here = proj[pl.ds(start + 8, TILE), :].reshape(TILE // Q, Q, LAT)
+        first = j == 0
+        first_ever = jnp.logical_and(first, l == 1)
+        before = node_rows(order(lax.rem(j + 3, 4)))
+        node_slot = lax.rem(l + jnp.where(jnp.logical_and(first, l > 1), 1, 0), 2)
+        next_slot = lax.rem(l + jnp.where(first, 0, 1), 2)
+        nodes = mesh[before, :]
+        sums = total[before, :]
+
+        at_recv = recv[slot, rows, :]
+        here = proj[slot, pl.ds(start + 8, TILE), :].reshape(TILE // Q, Q, LAT)
 
         def sender(k):
             if k == 0:
-                return proj[pl.ds(start + 16, TILE), :]
+                return proj[slot, pl.ds(start + 16, TILE), :]
             if k == 1:
-                return proj[rows, :]
+                return proj[slot, rows, :]
             shift = {2: Q - 1, 3: 1, 4: Q - 2, 5: 2}[k]
             return pltpu.roll(here, shift, 1).reshape(TILE, LAT)
 
@@ -283,7 +363,7 @@
         def stage_a(c):
             pair = edge[per * c:per * c + per, rows, :].reshape(CHUNK, LAT)
             old[c] = pair
-            terms = jnp.concatenate([sender(per * c + j) + at_recv for j in range(per)], axis=0)
+            terms = jnp.concatenate([sender(per * c + i) + at_recv for i in range(per)], axis=0)
             hid[c] = silu_twice(mm(pair, w_first) + terms)
 
         def stage_b(c):
@@ -293,81 +373,120 @@
             new = add_to(old[c], half_norm(upd[c]))
             edge[per * c:per * c + per, rows, :] = new.reshape(per, TILE, LAT)
             wide = new.astype(F32)
-            for j in range(per):
-                part = wide[j * TILE:(j + 1) * TILE]
+            for i in range(per):
+                part = wide[i * TILE:(i + 1) * TILE]
                 acc[0] = part if acc[0] is None else acc[0] + part
 
-        for c in range(chunks + LAG_C):
-            if c < chunks:
-                stage_a(c)
-            if LAG_B <= c < chunks + LAG_B:
-                stage_b(c - LAG_B)
-            if LAG_C <= c:
-                stage_c(c - LAG_C)
+        stage_a(0)
+        stage_a(1)
+        node_hid = silu_twice(mm(nodes, b_ni[node_slot, :LAT, :]) + mm(sums, b_ni[node_slot, LAT:, :]))
+        stage_b(0)
+        stage_a(2)
+        node_upd = mm(node_hid, b_no[node_slot])
+        stage_b(1)
+        stage_c(0)
+        stage_b(2)
+        node_new = add_to(nodes, half_norm(node_upd))
+        node_new = jnp.where(first_ever, nodes, node_new)
+        send_next = mm(node_new, b_ei[next_slot, LAT:2 * LAT, :])
+        recv_next = mm(node_new, b_ei[next_slot, 2 * LAT:, :])
+        stage_c(1)
+        stage_c(2)
         total[rows, :] = acc[0].astype(BF16)
-
-    def update_nodes(slot, last):
-        chunks = [pl.ds(c * 512, 512) for c in range(2)]
-        nodes = [mesh[rows, :] for rows in chunks]
-        hid = [silu_twice(mm(nodes[c], b_ni[slot, :LAT, :]) + mm(total[chunks[c], :], b_ni[slot, LAT:, :])) for c in range(2)]
-        upd = [mm(h, b_no[slot]) for h in hid]
-        for c in range(2):
-            new = add_to(nodes[c], half_norm(upd[c]))
-            if last:
-                for d, col in enumerate(LANE_COLS):
-                    turn[d, chunks[c], :] = new[:, col].astype(F32)
+        mesh[before, :] = node_new
+        proj[next_slot, pl.ds(order(lax.rem(j + 3, 4)) * TILE + 8, TILE), :] = send_next
+        recv[next_slot, before, :] = recv_next
+
+    def last_nodes(t):
+        rows = node_rows(t)
+        slot = LAYERS % 2
+        hid = silu_twice(mm(mesh[rows, :], b_ni[slot, :LAT, :]) + mm(total[rows, :], b_ni[slot, LAT:, :]))
+        mesh[rows, :] = add_to(mesh[rows, :], half_norm(mm(hid, b_no[slot])))
+
+    tile_r = TILE // Q
+
+    def parcels(t, sender):
+        rows = pl.ds(pl.multiple_of(t * tile_r, tile_r), tile_r)
+        made = []
+        for q in range(Q):
+            if sender:
+                slot = 2 * me + q % 2
+                made.append(Parcel(q // 2, out_buf.at[q, rows], h_out.at[me, q % 2, rows], o_send.at[t, q], o_recv.at[t, slot]))
             else:
-                mesh[chunks[c], :] = new
-                proj[pl.ds(8 + c * 512, 512), :] = mm(new, b_ei[1 - slot, LAT:2 * LAT, :])
-                recv[chunks[c], :] = mm(new, b_ei[1 - slot, 2 * LAT:, :])
-
-    def layer(l, last):
+                made.append(Parcel(q // 2, out_buf.at[q, rows], h_out.at[q // 2, q % 2, rows], o_send.at[t, q], o_recv.at[t, q]))
+        return made
+
+    def hand_over(t):
+        start = pl.multiple_of(t * TILE, TILE)
+        rows = pl.ds(start, TILE)
+        for c, col in enumerate(LANE_COLS):
+            turn[c, rows, :] = mesh[rows, col].astype(F32)
+        for c, col in enumerate(LANE_COLS):
+            for q in range(Q):
+                out_buf[q, pl.ds(pl.multiple_of(t * tile_r, tile_r), tile_r), col] = turn[c, pl.ds(start + q, tile_r, stride=Q), :].astype(BF16)
+        for parcel in parcels(t, True):
+            parcel.start()
+
+    def halo_copy(slot, side):
+        first, peer = ((NODES, right), (8, left))[side]
+        return pltpu.make_async_remote_copy(
+            src_ref=proj.at[slot, pl.ds(first, 8)],
+            dst_ref=halo.at[slot, side],
+            send_sem=s_sem.at[side],
+            recv_sem=r_sem.at[slot, side],
+            device_id={"gp": peer},
+            device_id_type=pl.DeviceIdType.MESH)
+
+    def layer(l, carry):
         slot = lax.rem(l, 2)
-        if not last:
-            for copy in weight_copies(l + 1, 1 - slot):
-                copy.start()
-        sends = [
-            pltpu.make_async_remote_copy(
-                src_ref=proj.at[pl.ds(first, 8)],
-                dst_ref=halo.at[slot, side],
-                send_sem=s_sem.at[side],
-                recv_sem=r_sem.at[slot, side],
-                device_id={"gp": peer},
-                device_id_type=pl.DeviceIdType.MESH)
-            for side, first, peer in ((0, NODES, right), (1, 8, left))]
-        for send in sends:
-            send.start()
-
-        def pair(base):
-            def body(i, carry):
-                edge_tile(slot, lax.rem(i + base, NODES // TILE))
-                return carry
-            lax.fori_loop(0, 2, body, 0)
-
-        pair(1)
-        for send in sends:
-            send.wait_recv()
-        below = halo[slot, 0]
-        above = halo[slot, 1]
-        proj[0:8, :] = jnp.where(me == 0, pltpu.roll(below, 1, 0), below)
-        proj[8 + NODES:16 + NODES, :] = jnp.where(me == ring - 1, pltpu.roll(above, Q - 1, 0), above)
-        pair(3)
-        for send in sends:
-            send.wait_send()
-        if not last:
-            for copy in weight_copies(l + 1, 1 - slot):
-                copy.wait()
-        update_nodes(slot, last)
-
-    def loop_body(l, carry):
-        layer(l, False)
+        start_all(edge_weights(l + 1))
+        halo_copy(slot, 1).start()
+
+        def body(j, carry):
+            @pl.when(j == 1)
+            def after_first():
+                halo_copy(slot, 0).start()
+                start_all(node_weights(l + 1))
+                wait_all(edge_weights(l + 1))
+
+            @pl.when(j == 2)
+            def border_below():
+                halo_copy(slot, 0).wait_recv()
+                below = halo[slot, 0]
+                proj[slot, 0:8, :] = jnp.where(me == 0, pltpu.roll(below, 1, 0), below)
+
+            @pl.when(j == 3)
+            def border_above():
+                halo_copy(slot, 1).wait_recv()
+                above = halo[slot, 1]
+                proj[slot, 8 + NODES:16 + NODES, :] = jnp.where(me == RING - 1, pltpu.roll(above, Q - 1, 0), above)
+
+            tile_step(l, j)
+
+            @pl.when(jnp.logical_and(l == LAYERS, j > 0))
+            def leave():
+                hand_over(order(j - 1))
+
+            return carry
+
+        lax.fori_loop(0, NODES // TILE, body, 0)
+        halo_copy(slot, 0).wait_send()
+        halo_copy(slot, 1).wait_send()
+        wait_all(node_weights(l + 1))
         return carry
 
-    lax.fori_loop(1, LAYERS, loop_body, 0)
-    layer(jnp.int32(LAYERS), True)
-    for c, col in enumerate(LANE_COLS):
-        for q in range(Q):
-            h_out[q, :, col] = turn[c, pl.ds(q, RLOC, stride=Q), :].astype(BF16)
+    lax.fori_loop(1, LAYERS + 1, layer, 0)
+    last_nodes(order(3))
+    hand_over(order(3))
+
+    def settle(t, carry):
+        for parcel in parcels(t, True):
+            parcel.wait_sent()
+        for parcel in parcels(t, False):
+            parcel.wait_arrived()
+        return carry
+
+    lax.fori_loop(0, NODES // TILE, settle, 0)
 
 
 def processor(h_in, lat, first_edge, w_edge_in, w_edge_out, w_node_in, w_node_out):
@@ -377,15 +496,16 @@
     return pl.pallas_call(
         functools.partial(proc_kernel, first_edge),
         in_specs=[vmem, hbm, hbm, hbm, hbm, hbm],
-        out_specs=vmem,
-        out_shape=jax.ShapeDtypeStruct((Q, RLOC, LAT), BF16),
+        out_specs=pl.BlockSpec(memory_space=pltpu.HBM),
+        out_shape=jax.ShapeDtypeStruct((RING, 2, RLOC, LAT), BF16),
         scratch_shapes=[
             pltpu.VMEM((OFFS, NODES, LAT), BF16),
             pltpu.VMEM((NODES, LAT), BF16),
-            pltpu.VMEM((NODES + 16, LAT), F32),
-            pltpu.VMEM((NODES, LAT), F32),
+            pltpu.VMEM((2, NODES + 16, LAT), F32),
+            pltpu.VMEM((2, NODES, LAT), F32),
             pltpu.VMEM((NODES, LAT), BF16),
             pltpu.VMEM((LAT // LANES, NODES, LANES), F32),
+            pltpu.VMEM((Q, RLOC, LAT), BF16),
             pltpu.VMEM((2, 2, 8, LAT), F32),
             pltpu.VMEM((2, 3 * LAT, LAT), BF16),
             pltpu.VMEM((2, LAT, LAT), BF16),
@@ -395,6 +515,8 @@
             pltpu.SemaphoreType.DMA((OFFS,)),
             pltpu.SemaphoreType.DMA((2,)),
             pltpu.SemaphoreType.DMA((2, 2)),
+            pltpu.SemaphoreType.DMA((NODES // TILE, Q)),
+            pltpu.SemaphoreType.DMA((NODES // TILE, Q)),
         ],
         compiler_params=pltpu.CompilerParams(collective_id=0, has_side_effects=True, vmem_limit_bytes=VMEM_LIMIT),
         cost_estimate=pl.CostEstimate(flops=2 * LAYERS * rows * LAT * LAT, bytes_accessed=60 * 2 ** 20, transcendentals=0),
@@ -431,8 +553,8 @@
         node_rows = padded(jnp.concatenate([node_rows[:, half:], head[:3]], axis=1))
         g2m_rows = padded(jnp.concatenate([g2m_rows[:, RATIO * half:]] + [head[3 + 4 * k:7 + 4 * k] for k in range(RATIO)], axis=1))
         feats = jnp.concatenate([node_rows, g2m_rows, padded(m2g_feat.astype(BF16).T)], axis=1)
-        lat = embed_static(feats, jnp.stack([padded(w_mesh_in), padded(w_eemb_in[0]), padded(w_eemb_in[1])]), w_embed_out[1:4], (mesh_dev, mesh_dev + grid_dev), "embed")
-        edge_lat = embed_static(edges, padded(w_eemb_in[2])[None], w_embed_out[4:5], (), "embed_edges")
+        lat = embed_static(feats, jnp.stack([padded(w_mesh_in), padded(w_eemb_in[0]), padded(w_eemb_in[1])]), w_embed_out, 1, (mesh_dev, mesh_dev + grid_dev), "embed")
+        edge_lat = embed_static(edges, padded(w_eemb_in[2])[None], w_embed_out, 4, (), "embed_edges")
 
         w_grid = jnp.concatenate([
             jnp.pad(w_grid_in[:VARS], ((0, FEAT_CUR - VARS), (0, 0))),
@@ -441,15 +563,13 @@
         w_final = jnp.pad(w_out_final, ((0, 0), (0, LANES - VARS)))
         last = w_edge_in.shape[0] - 1
         stats = norm_stats.T
-        enc_w = {"stats": stats, "w_grid": w_grid, "w_grid_out": w_embed_out[0], "wf": w_edge_in[0], "wf_out": w_edge_out[0], "wf_node": w_node_in[0], "wf_node_out": w_node_out[0], "w_self": w_grid_self}
-        dec_w = {"stats": stats, "wl": w_edge_in[last], "wl_out": w_edge_out[last], "wl_node": w_node_in[last], "wl_node_out": w_node_out[last], "w_hidden": w_out_hidden, "w_final": w_final}
+        enc_w = {"stats": stats, "w_grid": w_grid, "w_grid_out": (w_embed_out, 0), "wf": (w_edge_in, 0), "wf_out": (w_edge_out, 0), "wf_node": (w_node_in, 0), "wf_node_out": (w_node_out, 0), "w_self": w_grid_self}
+        dec_w = {"stats": stats, "wl": (w_edge_in, last), "wl_out": (w_edge_out, last), "wl_node": (w_node_in, last), "wl_node_out": (w_node_out, last), "w_hidden": w_out_hidden, "w_final": w_final}
         static_rows = padded(grid_static.T)
         force = [jnp.concatenate([padded(forcing[:, s, :].T), static_rows], axis=0) for s in range(2)]
 
         def process(h):
-            h = exchange(h).reshape(Q, RLOC, LAT)
-            h = processor(h, edge_lat, 0, w_edge_in, w_edge_out, w_node_in, w_node_out)
-            return exchange(h.reshape(ring, 2, RLOC, LAT))
+            return processor(h, edge_lat, 0, w_edge_in, w_edge_out, w_node_in, w_node_out)
 
         now = x_cur.T
         grid_lat, h = grid_call({"cur": now, "prev": x_prev.T, "force": force[0], "g2m": lat, "mesh": lat}, enc_w, False, True, "encode")

time: 562 us -> 510 us (0.907); the launches traced: 555 us -> 510 us
  blocking collectives: 37 us -> 0 us
  Pallas kernels: 456 us -> 482 us
  waiting for transfers between devices: 15.9 us -> 0.01 us
  local copies, waits for them, and re-layouts: 25 us -> 12.2 us
  starting transfers between devices: 13.7 us -> 6.08 us
    all_to_all x2 -> x0, blocking collectives: 37 us -> none  [exchange(): return lax.all_to_all(x, 'gp', 0, 0)]
    all_to_all x3 -> x1, waiting for transfers between devices: 15.9 us -> 0.01 us  [exchange(): return lax.all_to_all(x, 'gp', 0, 0)]
    pallas_call x3, Pallas kernels: 95.8 us -> 111 us  [grid_call(): pl.pallas_call(functools.partial(grid_kernel, tuple(names), decode, encod...]
    pallas_call x2, Pallas kernels: 337 us -> 348 us  [processor(): pl.pallas_call(functools.partial(proc_kernel, first_edge), in_specs=[vmem...]
    squeeze x3 -> x0, local copies, waits for them, and re-layouts: 9.89 us -> none  [the longest x1 3.87 us: local_run(): w_edge_in[last]]
    all_to_all x3 -> x1, starting transfers between devices: 10.9 us -> 3.27 us  [exchange(): return lax.all_to_all(x, 'gp', 0, 0)]
  transfers between devices with their start and end apart: 4 -> 2, of which waited for: 2 -> 0; matrix products, arithmetic and copies ran while one was open for 5% -> 3% of each run, Pallas kernels for 9% -> 9%
where the time goes in v1:
time: 510 us
  Pallas kernels  482 us (95%)
  local copies, waits for them, and re-layouts  12.2 us (2%)
  other arithmetic  8.08 us (2%)
  starting transfers between devices  6.08 us (1%)
    pallas_call x2, Pallas kernels, processor(): pl.pallas_call(functools.partial(proc_kernel, first_edge), in_specs=[vmem...  348 us
    pallas_call x3, Pallas kernels, grid_call(): pl.pallas_call(functools.partial(grid_kernel, tuple(names), decode, encod...  111 us
    pallas_call x2, Pallas kernels, embed_static(): pl.pallas_call(embed_kernel, grid=(rows // block,), in_specs=[pl.BlockSpe...  22.9 us
  transfers between devices with their start and end apart: 2, of which 0 were waited for; matrix products, arithmetic and copies ran while one was open for 3% of the time, Pallas kernels for 9%

profile of v1, /device:TPU:0, one launch (start us, length us, event | category | flops | bytes accessed | tf_op | source)
XLA Modules:
  0.0 509.5 jit_solution(4693687892898450180)
XLA Ops:
  0.6 0.7 convert_bitcast_fusion.3
  1.4 0.9 convert_bitcast_fusion.2
  2.2 0.2 concatenate.26
  2.5 2.8 collective-permute-start
  5.3 0.9 convert_bitcast_fusion
  6.2 0.7 copy.47
  6.9 3.3 all-to-all-start
  10.2 0.8 fusion.17
  11.0 0.9 slice.88
  11.9 0.7 pad_bitcast_fusion.3
  12.6 0.7 slice_bitcast_fusion
  13.3 0.9 convert_bitcast_fusion.1
  14.2 1.0 slice_select_fusion
  15.1 1.2 fusion.18
  16.3 0.1 copy_bitcast_fusion
  16.4 0.6 pad_maximum_fusion.1.w_in_ref
  17.0 1.7 select_maximum_fusion
  18.8 0.7 fusion.10.refs_6_.refs_14_
  19.5 0.6 pad_bitcast_fusion.w_in_ref
  20.1 1.4 copy.46
  21.5 1.0 copy.52
  22.5 0.7 pad.72.refs_13_.refs_10_
  23.2 0.0 collective-permute-done
  23.3 0.7 fusion.13.x_ref
  23.9 13.5 %embed.1.refs_3_.refs_4_.refs_5_.refs_6_ = bf16[9216,512]{1,0:T(8,128)(2,1)} custom-call(bf16[8,9216]{1,0:T(8,128)(2,1)} %fusion.13.x_ref, bf16[3,8,512]{2,1,0:T(8,128)(2,1)} %pad_maximum_fusion.1.w_in_ref, bf16[5,512,512]{2,1,0:T(8,128)(2,1)} %refs_15_.1), custom_call_target="tpu_custom_call" | custom-call | flops 14495514624 | bytes 9437184 | tf_op jit(solution)/shard_map/embed/pallas_call | solution.py:66
  37.4 34.3 %encode.1 = (bf16[4096,512]{1,0:T(8,128)(2,1)}, bf16[8,128,512]{2,1,0:T(8,128)(2,1)}) custom-call(f32[83,4096]{1,0:T(8,128)} %bitcast.42, f32[83,4096]{1,0:T(8,128)} %bitcast.45, f32[16,4096]{1,0:T(8,128)} %get-tuple-element.17.refs_2_, bf16[9216,512]{1,0:T(8,128)(2,1)} %embed.1.refs_3_.refs_4_.refs_5_.refs_6_, ...), custom_call_target="tpu_custom_call" | custom-call | flops 15032385536 | bytes 16777216 | tf_op jit(solution)/shard_map/encode/pallas_call | solution.py:275
  71.7 0.0 all-to-all-done
  71.8 0.1 reshape.18
  71.9 0.4 copy.50
  72.3 0.9 reshape.19
  73.2 0.7 pad.69.x_ref
  73.9 9.4 %embed_edges.1.lat = bf16[6144,512]{1,0:T(8,128)(2,1)} custom-call(bf16[8,6144]{1,0:T(8,128)(2,1)} %pad.69.x_ref, bf16[1,8,512]{2,1,0:T(8,128)(2,1)} %pad_bitcast_fusion.w_in_ref, bf16[5,512,512]{2,1,0:T(8,128)(2,1)} %refs_15_.1), custom_call_target="tpu_custom_call" | custom-call | flops 9663676416 | bytes 6291456 | tf_op jit(solution)/shard_map/embed_edges/pallas_call | solution.py:66
  83.3 174.1 %processor.2.refs_1_ = bf16[4,2,128,512]{3,2,1,0:T(8,128)(2,1)} custom-call(bf16[8,128,512]{2,1,0:T(8,128)(2,1)} %get-tuple-element.7.h_in, bf16[6144,512]{1,0:T(8,128)(2,1)} %embed_edges.1.lat, bf16[14,1536,512]{2,1,0:T(8,128)(2,1)} %refs_5_.1, bf16[14,512,512]{2,1,0:T(8,128)(2,1)} %refs_6_.1, bf16[14,1024,512]{2,1,0:T(8,128)(2,1)} %refs_7_.3, ...), custom_call_target="tpu_custom_call" | custom-call | flops 128849018880 | bytes 62914560 | tf_op jit(solution)/shard_map/processor/pallas_call | solution.py:496
  257.4 53.5 %decode_encode.1 = (f32[83,4096]{1,0:T(8,128)}, bf16[4096,512]{1,0:T(8,128)(2,1)}, bf16[8,128,512]{2,1,0:T(8,128)(2,1)}) custom-call(f32[83,4096]{1,0:T(8,128)} %bitcast.43, bf16[4,2,128,512]{3,2,1,0:T(8,128)(2,1)} %processor.2.refs_1_, bf16[4096,512]{1,0:T(8,128)(2,1)} %get-tuple-element.8.refs_2_, bf16[9216,512]{1,0:T(8,128)(2,1)} %embed.1.refs_3_.refs_4_.refs_5_.refs_6_, ...), custom_call_target="tpu_custom_call" | custom-call | flops 30064771072 | bytes 16777216 | tf_op jit(solution)/shard_map/decode_encode/pallas_call | solution.py:275
  310.9 174.1 %processor.3.refs_1_ = bf16[4,2,128,512]{3,2,1,0:T(8,128)(2,1)} custom-call(bf16[8,128,512]{2,1,0:T(8,128)(2,1)} %get-tuple-element.10.h_in, bf16[6144,512]{1,0:T(8,128)(2,1)} %embed_edges.1.lat, bf16[14,1536,512]{2,1,0:T(8,128)(2,1)} %refs_5_.1, bf16[14,512,512]{2,1,0:T(8,128)(2,1)} %refs_6_.1, bf16[14,1024,512]{2,1,0:T(8,128)(2,1)} %refs_7_.3, ...), custom_call_target="tpu_custom_call" | custom-call | flops 128849018880 | bytes 62914560 | tf_op jit(solution)/shard_map/processor/pallas_call | solution.py:496
  485.0 0.0 copy-start
  485.0 23.4 %decode.1 = f32[83,4096]{1,0:T(8,128)} custom-call(f32[83,4096]{1,0:T(8,128)} %get-tuple-element.9.refs_0_, bf16[4,2,128,512]{3,2,1,0:T(8,128)(2,1)} %processor.3.refs_1_, bf16[4096,512]{1,0:T(8,128)(2,1)} %get-tuple-element.11.refs_2_, bf16[9216,512]{1,0:T(8,128)(2,1)} %embed.1.refs_3_.refs_4_.refs_5_.refs_6_, f32[83,4]{1,0:T(8,128)} %bitcast.49, ...), custom_call_target="tpu_custom_call" | custom-call | flops 15032385536 | bytes 16777216 | tf_op jit(solution)/shard_map/decode/pallas_call | solution.py:275
  508.4 0.0 copy-done
  508.4 1.1 copy.62
  (16 shorter events, 0.2 us)
Async XLA Ops:
  2.5 20.7 %collective-permute-start = (bf16[19,512]{1,0:T(8,128)(2,1)S(1)}, bf16[19,512]{1,0:T(8,128)(2,1)S(1)}, u32[]{:S(2)}, u32[]{:S(2)}) collective-permute-start(bf16[19,512]{1,0:T(8,128)(2,1)S(1)} %concatenate.26), channel_id=1, source_target_pairs={{0,3},{1,0},{2,1},{3,2},{4,7},{5,4},{6,5},{7,6}} | collective-permute-start | bytes 58376 | tf_op jit(solution)/shard_map/ppermute | solution.py:552
  6.9 64.9 %all-to-all-start = ((bf16[4,24,2,128]{3,2,1,0:T(2,128)(2,1)}), bf16[4,24,2,128]{3,2,1,0:T(2,128)(2,1)S(1)}, u32[]{:S(2)}, u32[]{:S(2)}) async-start(bf16[4,24,2,128]{3,2,1,0:T(2,128)(2,1)} %copy.47), calls=%async_computation | async-start | bytes 98304 | tf_op jit(solution)/shard_map/all_to_all | solution.py:534
  485.0 23.4 %copy-start = (f32[83,4096]{1,0:T(8,128)S(1)}, f32[83,4096]{1,0:T(8,128)}, u32[]{:S(2)}) copy-start(f32[83,4096]{1,0:T(8,128)} %get-tuple-element.9.refs_0_) | copy-start | bytes 4079620
